TPU v7x, 32 devices: a whole 2x2x4 slice. The times are simulated.
32 devices in a mesh: batch: 2 (over x), items: 16 (over z, y, core).
Axes of the slice: x: 2, y: 2, z: 4, core: 2. Of those that a mesh axis runs over, the one named last changes fastest.
Arguments:
- users: bfloat16 [1280, 256], P(('batch', 'items')), may hold values from -6 to 6
- items: bfloat16 [8192, 256], P(('batch', 'items')), may hold values from -6 to 6
- pos_ids: int32 [1280], P(('batch', 'items')), may hold values from 0 to 8191
Outputs:
- loss: float32 [1280], P(('batch', 'items'))
- user_grad: float32 [1280, 256], P(('batch', 'items'))
- item_grad: float32 [8192, 256], P(('batch', 'items'))
All inputs are finite; a program needn't handle non-finite values.
Results may differ from a plain program's by a relative error of at most 0.0015.
Values may be sent and summed in bfloat16 or wider, within the bound.
No kernel may reach another device: no remote copies, remote signals or barrier semaphores. Data moves between devices by JAX's collectives and lax.ppermute only.
A program may use at most 64 MiB of HBM per device.

v0:
```python
import jax
import jax.numpy as jnp
from jax import lax
from jax.sharding import PartitionSpec as P


def swap(value, axis, mask):
    count = lax.axis_size(axis)
    return lax.ppermute(value, axis, [(i, i ^ mask) for i in range(count)])


def user_steps(count):
    bits = [1 << k for k in range(count.bit_length() - 1)][1:]
    steps = [(b, b) for b in bits[1:]]
    return steps + [(b, b) for b in bits[:1]]


def doubled(mine, theirs, upper):
    return jnp.where(
        upper, jnp.concatenate([theirs, mine], 0), jnp.concatenate([mine, theirs], 0)
    )


def local(users, items, pos_ids):
    f32, bf16 = jnp.float32, jnp.bfloat16
    own, width = users.shape
    per_bank = items.shape[0]
    count = lax.axis_size("items")
    here = lax.axis_index("items")
    group = lax.axis_index("batch")
    steps = user_steps(count)
    block = -(-(own + 1) // 16) * 16

    ids_row = jnp.concatenate(
        [pos_ids // 256, pos_ids % 256, jnp.zeros((width - 2 * own,), jnp.int32)]
    ).astype(bf16)
    seen = jnp.concatenate([users, ids_row[None], jnp.zeros((block - own - 1, width), bf16)], 0)
    half_bank = jnp.concatenate([items, swap(items, "batch", 1)], 0)
    for bit, mask in steps:
        theirs = swap(seen, "items", mask)
        seen = doubled(seen, theirs, (here & bit) != 0)
    bank = jnp.concatenate([half_bank, swap(half_bank, "items", 1)], 0)
    rows = seen.shape[0]
    blocks = rows // block

    pairs = seen.reshape(blocks, block, width)[:, own, : 2 * own].astype(jnp.int32)
    ids = pairs[:, :own] * 256 + pairs[:, own:]
    owner = ids // per_bank
    at = owner % count
    slot = ((at ^ here) & 1) * 2 + ((owner // count) ^ group)
    column = jnp.where((at >> 1) == (here >> 1), slot * per_bank + ids % per_bank, -1)
    column = jnp.pad(column, ((0, 0), (0, block - own)), constant_values=-1).reshape(rows)
    cols = jnp.arange(bank.shape[0], dtype=jnp.int32)
    real = (jnp.arange(rows, dtype=jnp.int32) % block) < own

    logit = lax.dot_general(seen, bank, (((1,), (1,)), ((), ())), preferred_element_type=f32)
    match = column[:, None] == cols[None, :]
    peak = jnp.max(logit, axis=1)
    power = jnp.exp(logit - peak[:, None])
    total = jnp.sum(power, axis=1)
    positive = jnp.sum(jnp.where(match, logit, 0.0), axis=1)
    high = power.astype(bf16)
    low = (power - high.astype(f32)).astype(bf16)
    acc = jnp.dot(high, bank, preferred_element_type=f32) + jnp.dot(
        low, bank, preferred_element_type=f32
    )
    pick = jnp.dot(match.astype(bf16), bank, preferred_element_type=f32).astype(bf16)

    for n, (bit, mask) in enumerate(reversed(steps)):
        upper = ((here & bit) != 0).astype(jnp.int32)
        half = acc.shape[0] // 2
        stats = swap(jnp.stack([peak, total, positive]), "items", mask)
        give = (1 - upper) * half
        wire = f32 if n == len(steps) - 1 else bf16
        sent = jnp.concatenate(
            [
                lax.dynamic_slice_in_dim(acc, give, half, 0).astype(wire),
                lax.dynamic_slice_in_dim(pick, give, half, 0).astype(wire),
            ],
            0,
        )
        got = swap(sent, "items", mask)
        top = jnp.maximum(peak, stats[0])
        scale_mine = jnp.exp(peak - top)
        scale_theirs = jnp.exp(stats[0] - top)
        total = total * scale_mine + stats[1] * scale_theirs
        positive = positive + stats[2]
        peak = top
        keep = upper * half
        base = keep if acc.shape[0] == rows else base + keep
        mine = lax.dynamic_slice_in_dim(scale_mine, base, half, 0)
        theirs = lax.dynamic_slice_in_dim(scale_theirs, base, half, 0)
        acc = (
            lax.dynamic_slice_in_dim(acc, keep, half, 0) * mine[:, None]
            + got[:half].astype(f32) * theirs[:, None]
        )
        pick = lax.dynamic_slice_in_dim(pick, keep, half, 0) + got[half:].astype(bf16)

    lse = peak + jnp.log(total)
    last = lambda v: lax.dynamic_slice_in_dim(v, base, block, 0)[:own]
    loss = last(lse) - last(positive)
    user_grad = acc[:own] / last(total)[:, None] - pick[:own].astype(f32)

    weights = (jnp.exp(logit - lse[:, None]) - jnp.where(match, 1.0, 0.0)).astype(bf16)
    clean = jnp.where(real[:, None], seen, jnp.zeros((), bf16))
    grad = lax.dot_general(weights, clean, (((0,), (0,)), ((), ())), preferred_element_type=f32)
    near = 2 * per_bank
    grad = grad[:near] + swap(grad[near:], "items", 1)
    item_grad = grad[:per_bank] + swap(grad[per_bank:].astype(bf16), "batch", 1).astype(f32)
    return (loss, user_grad, item_grad)


def solution(mesh):
    placed = (P(("batch", "items"), None), P(("batch", "items"), None), P(("batch", "items")))
    return jax.shard_map(
        local,
        mesh=mesh,
        in_specs=placed,
        out_specs=(P(("batch", "items")), P(("batch", "items"), None), P(("batch", "items"), None)),
        check_vma=False,
    )
```

profile of v0, /device:TPU:0, one launch (start us, length us, event | category | flops | bytes accessed | tf_op | source)
XLA Modules:
  0.0 53.3 jit_solution(8712053718108929355)
XLA Ops:
  0.6 0.7 %convert_bitcast_fusion = (bf16[1,40]{1,0:T(2,128)(2,1)S(1)}, bf16[1,40]{1,0:T(2,128)(2,1)S(1)}) fusion(s32[40]{0:T(128)} %param.5), kind=kLoop, calls=%fused_computation.116 | loop fusion | flops 840 | bytes 320 | tf_op jit(solution)/shard_map/concatenate | solution.py:34
  1.3 0.8 %pad_maximum_fusion.4 = bf16[48,256]{1,0:T(8,128)(2,1)S(1)} fusion(bf16[7,256]{1,0:T(8,128)(2,1)S(1)} %broadcast_in_dim.25, bf16[1,176]{1,0:T(2,128)(2,1)S(1)} %broadcast_in_dim.24, bf16[1,40]{1,0:T(2,128)(2,1)S(1)} %get-tuple-element.36, bf16[1,40]{1,0:T(2,128)(2,1)S(1)} %get-tuple-element.35, bf16[40,256]{1,0:T(8,128)(2,1)} %param.3), kind=kLoop, calls=%fused_computation.44 | loop fusion | flops 122880 | bytes 49152 | tf_op jit(solution)/shard_map/concatenate | solution.py:37
  2.1 3.1 %collective-permute-start = (bf16[48,256]{1,0:T(8,128)(2,1)S(1)}, bf16[48,256]{1,0:T(8,128)(2,1)S(1)}, u32[]{:S(2)}, u32[]{:S(2)}) collective-permute-start(bf16[48,256]{1,0:T(8,128)(2,1)S(1)} %pad_maximum_fusion.4), channel_id=1, source_target_pairs={{0,4},{1,5},{2,6},{3,7},{4,0},{5,1},{6,2},{7,3},{8,12},{9,13},{10,... | collective-permute-start | bytes 73736 | tf_op jit(solution)/shard_map/ppermute | solution.py:9
  5.2 1.5 %collective-permute-start.3 = (bf16[256,256]{1,0:T(8,128)(2,1)}, bf16[256,256]{1,0:T(8,128)(2,1)S(1)}, u32[]{:S(2)}, u32[]{:S(2)}) collective-permute-start(bf16[256,256]{1,0:T(8,128)(2,1)} %param.4), channel_id=1, source_target_pairs={{0,16},{16,0},{1,17},{17,1},{2,18},{18,2},{3,19},{19,3},{4,20},{20... | collective-permute-start | bytes 393224 | tf_op jit(solution)/shard_map/ppermute | solution.py:9
  6.7 0.9 %constant_dynamic-update-slice_fusion.2 = bf16[1024,256]{1,0:T(8,128)(2,1)S(1)} fusion(bf16[256,256]{1,0:T(8,128)(2,1)} %param.4), kind=kLoop, calls=%fused_computation.49 | loop fusion | bytes 262144
  7.6 0.9 %maximum_select_fusion.2 = bf16[96,256]{1,0:T(8,128)(2,1)S(1)} fusion(bf16[7,256]{1,0:T(8,128)(2,1)S(1)} %broadcast_in_dim.25, bf16[1,176]{1,0:T(2,128)(2,1)S(1)} %broadcast_in_dim.24, bf16[1,40]{1,0:T(2,128)(2,1)S(1)} %get-tuple-element.36, bf16[1,40]{1,0:T(2,128)(2,1)S(1)} %get-tuple-element.35, bf16[40,256]{1,0:T(8,128)(2,1)} %param.3, ...), kind=kLoop, calls=%fused_computation.37 | loop fusion | flops 614400 | bytes 98305 | tf_op jit(solution)/shard_map/jit(_where)/select_n | solution.py:19
  8.5 2.6 %collective-permute-start.1 = (bf16[96,256]{1,0:T(8,128)(2,1)S(1)}, bf16[96,256]{1,0:T(8,128)(2,1)S(1)}, u32[]{:S(2)}, u32[]{:S(2)}) collective-permute-start(bf16[96,256]{1,0:T(8,128)(2,1)S(1)} %maximum_select_fusion.2), channel_id=1, source_target_pairs={{0,8},{1,9},{2,10},{3,11},{4,12},{5,13},{6,14},{7,15},{8,0},{9,1},... | collective-permute-start | bytes 147464 | tf_op jit(solution)/shard_map/ppermute | solution.py:9
  11.1 2.4 %collective-permute-done.1 = bf16[96,256]{1,0:T(8,128)(2,1)S(1)} collective-permute-done((bf16[96,256]{1,0:T(8,128)(2,1)S(1)}, bf16[96,256]{1,0:T(8,128)(2,1)S(1)}, u32[]{:S(2)}, u32[]{:S(2)}) %collective-permute-start.1) | collective-permute-done | bytes 49184 | tf_op jit(solution)/shard_map/ppermute | solution.py:9
  13.6 1.6 %collective-permute-start.2 = (bf16[192,256]{1,0:T(8,128)(2,1)S(1)}, bf16[192,256]{1,0:T(8,128)(2,1)S(1)}, u32[]{:S(2)}, u32[]{:S(2)}) collective-permute-start(bf16[192,256]{1,0:T(8,128)(2,1)S(1)} %maximum_select_fusion.1), channel_id=1, source_target_pairs={{0,2},{1,3},{2,0},{3,1},{4,6},{5,7},{6,4},{7,5},{8,10},{9,11},{10,... | collective-permute-start | bytes 294920 | tf_op jit(solution)/shard_map/ppermute | solution.py:9
  15.1 0.9 %pad_maximum_fusion = bf16[512,256]{1,0:T(8,128)(2,1)S(1)} fusion(bf16[256,256]{1,0:T(8,128)(2,1)S(1)} %collective-permute-done.3, bf16[256,256]{1,0:T(8,128)(2,1)} %param.4), kind=kLoop, calls=%fused_computation.22 | loop fusion | flops 524288 | bytes 524288 | tf_op jit(solution)/shard_map/concatenate | solution.py:38
  16.2 2.1 %collective-permute-done.2 = bf16[192,256]{1,0:T(8,128)(2,1)S(1)} collective-permute-done((bf16[192,256]{1,0:T(8,128)(2,1)S(1)}, bf16[192,256]{1,0:T(8,128)(2,1)S(1)}, u32[]{:S(2)}, u32[]{:S(2)}) %collective-permute-start.2) | collective-permute-done | bytes 98336 | tf_op jit(solution)/shard_map/ppermute | solution.py:9
  18.5 0.5 fusion.42
  19.0 0.4 fusion.5
  19.5 0.5 fusion.2
  20.0 1.6 %collective-permute-start.5 = (f32[3,384]{1,0:T(4,128)S(1)}, f32[3,384]{1,0:T(4,128)S(1)}, u32[]{:S(2)}, u32[]{:S(2)}) collective-permute-start(f32[3,384]{1,0:T(4,128)S(1)} %pad_maximum_fusion.5), channel_id=1, source_target_pairs={{0,2},{1,3},{2,0},{3,1},{4,6},{5,7},{6,4},{7,5},{8,10},{9,11},{10,... | collective-permute-start | bytes 13832 | tf_op jit(solution)/shard_map/ppermute | solution.py:9
  22.0 0.4 fusion.3
  22.5 1.2 %collective-permute-done.5 = f32[3,384]{1,0:T(4,128)S(1)} collective-permute-done((f32[3,384]{1,0:T(4,128)S(1)}, f32[3,384]{1,0:T(4,128)S(1)}, u32[]{:S(2)}, u32[]{:S(2)}) %collective-permute-start.5) | collective-permute-done | bytes 4640 | tf_op jit(solution)/shard_map/ppermute | solution.py:9
  23.8 2.8 %collective-permute-start.6 = (f32[3,384]{1,0:T(4,128)S(1)}, f32[3,384]{1,0:T(4,128)S(1)}, u32[]{:S(2)}, u32[]{:S(2)}) collective-permute-start(f32[3,384]{1,0:T(4,128)S(1)} %pad_maximum_fusion.6), channel_id=1, source_target_pairs={{0,8},{1,9},{2,10},{3,11},{4,12},{5,13},{6,14},{7,15},{8,0},{9,1},... | collective-permute-start | bytes 13832 | tf_op jit(solution)/shard_map/ppermute | solution.py:9
  26.5 1.8 %collective-permute-done.6 = f32[3,384]{1,0:T(4,128)S(1)} collective-permute-done((f32[3,384]{1,0:T(4,128)S(1)}, f32[3,384]{1,0:T(4,128)S(1)}, u32[]{:S(2)}, u32[]{:S(2)}) %collective-permute-start.6) | collective-permute-done | bytes 4640 | tf_op jit(solution)/shard_map/ppermute | solution.py:9
  28.4 1.6 %collective-permute-start.7 = (f32[3,384]{1,0:T(4,128)S(1)}, f32[3,384]{1,0:T(4,128)S(1)}, u32[]{:S(2)}, u32[]{:S(2)}) collective-permute-start(f32[3,384]{1,0:T(4,128)S(1)} %pad_maximum_fusion.7), channel_id=1, source_target_pairs={{0,4},{1,5},{2,6},{3,7},{4,0},{5,1},{6,2},{7,3},{8,12},{9,13},{10,... | collective-permute-start | bytes 13832 | tf_op jit(solution)/shard_map/ppermute | solution.py:9
  30.0 1.6 %collective-permute-start.8 = (bf16[384,256]{1,0:T(8,128)(2,1)S(1)}, bf16[384,256]{1,0:T(8,128)(2,1)S(1)}, u32[]{:S(2)}, u32[]{:S(2)}) collective-permute-start(bf16[384,256]{1,0:T(8,128)(2,1)S(1)} %pad_maximum_fusion.1), channel_id=1, source_target_pairs={{0,2},{1,3},{2,0},{3,1},{4,6},{5,7},{6,4},{7,5},{8,10},{9,11},{10,... | collective-permute-start | bytes 589832 | tf_op jit(solution)/shard_map/ppermute | solution.py:9
  31.6 0.5 collective-permute-done.7
  32.3 3.5 %collective-permute-done.8 = bf16[384,256]{1,0:T(8,128)(2,1)S(1)} collective-permute-done((bf16[384,256]{1,0:T(8,128)(2,1)S(1)}, bf16[384,256]{1,0:T(8,128)(2,1)S(1)}, u32[]{:S(2)}, u32[]{:S(2)}) %collective-permute-start.8) | collective-permute-done | bytes 196640 | tf_op jit(solution)/shard_map/ppermute | solution.py:9
  36.0 3.0 %collective-permute-start.9 = (bf16[192,256]{1,0:T(8,128)(2,1)S(1)}, bf16[192,256]{1,0:T(8,128)(2,1)S(1)}, u32[]{:S(2)}, u32[]{:S(2)}) collective-permute-start(bf16[192,256]{1,0:T(8,128)(2,1)S(1)} %pad_maximum_fusion.2), channel_id=1, source_target_pairs={{0,8},{1,9},{2,10},{3,11},{4,12},{5,13},{6,14},{7,15},{8,0},{9,1},... | collective-permute-start | bytes 294920 | tf_op jit(solution)/shard_map/ppermute | solution.py:9
  39.0 0.7 %fusion.6 = f32[1024,256]{1,0:T(8,128)S(1)} fusion(f32[384,1024]{1,0:T(8,128)S(1)} %get-tuple-element.38, f32[384]{0:T(512)S(1)} %get-tuple-element.14, s32[384]{0:T(512)S(1)} %eq.30, bf16[384,256]{1,0:T(8,128)(2,1)S(1)} %maximum_select_fusion, pred[384]{0:T(512)(128)(4,1)S(1)} %fusion.32), kind=kOutput, calls=%fused_computation.11 | convolution fusion | flops 203390976 | bytes 2821504 | tf_op jit(solution)/shard_map/dot_general | solution.py:106
  40.1 2.4 %collective-permute-done.9 = bf16[192,256]{1,0:T(8,128)(2,1)S(1)} collective-permute-done((bf16[192,256]{1,0:T(8,128)(2,1)S(1)}, bf16[192,256]{1,0:T(8,128)(2,1)S(1)}, u32[]{:S(2)}, u32[]{:S(2)}) %collective-permute-start.9) | collective-permute-done | bytes 98336 | tf_op jit(solution)/shard_map/ppermute | solution.py:9
  42.8 0.5 slice_subtract_fusion
  43.5 3.9 %collective-permute-done.10 = f32[96,256]{1,0:T(8,128)S(1)} collective-permute-done((f32[96,256]{1,0:T(8,128)S(1)}, f32[96,256]{1,0:T(8,128)S(1)}, u32[]{:S(2)}, u32[]{:S(2)}) %collective-permute-start.10) | collective-permute-done | bytes 98336 | tf_op jit(solution)/shard_map/ppermute | solution.py:9
  47.5 1.4 %collective-permute-start.12 = (bf16[256,256]{1,0:T(8,128)(2,1)S(1)}, bf16[256,256]{1,0:T(8,128)(2,1)S(1)}, u32[]{:S(2)}, u32[]{:S(2)}) collective-permute-start(bf16[256,256]{1,0:T(8,128)(2,1)S(1)} %slice.184), channel_id=1, source_target_pairs={{0,16},{16,0},{1,17},{17,1},{2,18},{18,2},{3,19},{19,3},{4,20},{20... | collective-permute-start | bytes 393224 | tf_op jit(solution)/shard_map/ppermute | solution.py:9
  48.9 0.7 %fusion.19 = f32[40,256]{1,0:T(8,128)} fusion(f32[48,256]{1,0:T(8,128)S(1)} %slice.127, f32[96,256]{1,0:T(8,128)S(1)} %multiply_add_fusion.1, s32[]{:T(128)S(6)} %mul.150, bf16[48,256]{1,0:T(8,128)(2,1)S(1)} %slice.131, bf16[96,256]{1,0:T(8,128)(2,1)S(1)} %slice_add_fusion.3, f32[40]{0:T(128)S(1)} %bitcast.16, f32[40]{0:T(128)S(1)} %bitcast.17, ...), kind=kLoop, calls=%fused_computation.42 | loop fusion | flops 92160 | bytes 164324 | tf_op jit(solution)/shard_map/sub | solution.py:102
  49.6 3.0 %collective-permute-done.12 = bf16[256,256]{1,0:T(8,128)(2,1)S(1)} collective-permute-done((bf16[256,256]{1,0:T(8,128)(2,1)S(1)}, bf16[256,256]{1,0:T(8,128)(2,1)S(1)}, u32[]{:S(2)}, u32[]{:S(2)}) %collective-permute-start.12) | collective-permute-done | bytes 131104 | tf_op jit(solution)/shard_map/ppermute | solution.py:9
  52.6 0.7 %slice_add_fusion.1 = f32[256,256]{1,0:T(8,128)} fusion(f32[512,256]{1,0:T(8,128)S(1)} %slice_add_fusion, bf16[256,256]{1,0:T(8,128)(2,1)S(1)} %collective-permute-done.12), kind=kLoop, calls=%fused_computation.21 | loop fusion | flops 131072 | bytes 655360 | tf_op jit(solution)/shard_map/add | solution.py:109
  (56 shorter events, 2.3 us)
Async XLA Ops:
  2.1 5.5 %collective-permute-start = (bf16[48,256]{1,0:T(8,128)(2,1)S(1)}, bf16[48,256]{1,0:T(8,128)(2,1)S(1)}, u32[]{:S(2)}, u32[]{:S(2)}) collective-permute-start(bf16[48,256]{1,0:T(8,128)(2,1)S(1)} %pad_maximum_fusion.4), channel_id=1, source_target_pairs={{0,4},{1,5},{2,6},{3,7},{4,0},{5,1},{6,2},{7,3},{8,12},{9,13},{10,... | collective-permute-start | bytes 73736 | tf_op jit(solution)/shard_map/ppermute | solution.py:9
  5.2 10.0 %collective-permute-start.3 = (bf16[256,256]{1,0:T(8,128)(2,1)}, bf16[256,256]{1,0:T(8,128)(2,1)S(1)}, u32[]{:S(2)}, u32[]{:S(2)}) collective-permute-start(bf16[256,256]{1,0:T(8,128)(2,1)} %param.4), channel_id=1, source_target_pairs={{0,16},{16,0},{1,17},{17,1},{2,18},{18,2},{3,19},{19,3},{4,20},{20... | collective-permute-start | bytes 393224 | tf_op jit(solution)/shard_map/ppermute | solution.py:9
  8.5 5.0 %collective-permute-start.1 = (bf16[96,256]{1,0:T(8,128)(2,1)S(1)}, bf16[96,256]{1,0:T(8,128)(2,1)S(1)}, u32[]{:S(2)}, u32[]{:S(2)}) collective-permute-start(bf16[96,256]{1,0:T(8,128)(2,1)S(1)} %maximum_select_fusion.2), channel_id=1, source_target_pairs={{0,8},{1,9},{2,10},{3,11},{4,12},{5,13},{6,14},{7,15},{8,0},{9,1},... | collective-permute-start | bytes 147464 | tf_op jit(solution)/shard_map/ppermute | solution.py:9
  13.6 4.7 %collective-permute-start.2 = (bf16[192,256]{1,0:T(8,128)(2,1)S(1)}, bf16[192,256]{1,0:T(8,128)(2,1)S(1)}, u32[]{:S(2)}, u32[]{:S(2)}) collective-permute-start(bf16[192,256]{1,0:T(8,128)(2,1)S(1)} %maximum_select_fusion.1), channel_id=1, source_target_pairs={{0,2},{1,3},{2,0},{3,1},{4,6},{5,7},{6,4},{7,5},{8,10},{9,11},{10,... | collective-permute-start | bytes 294920 | tf_op jit(solution)/shard_map/ppermute | solution.py:9
  16.1 2.4 %collective-permute-start.4 = (bf16[512,256]{1,0:T(8,128)(2,1)S(1)}, bf16[512,256]{1,0:T(8,128)(2,1)S(1)}, u32[]{:S(2)}, u32[]{:S(2)}) collective-permute-start(bf16[512,256]{1,0:T(8,128)(2,1)S(1)} %pad_maximum_fusion), channel_id=1, source_target_pairs={{0,1},{1,0},{2,3},{3,2},{4,5},{5,4},{6,7},{7,6},{8,9},{9,8},{10,11... | collective-permute-start | bytes 786440 | tf_op jit(solution)/shard_map/ppermute | solution.py:9
  20.0 3.7 %collective-permute-start.5 = (f32[3,384]{1,0:T(4,128)S(1)}, f32[3,384]{1,0:T(4,128)S(1)}, u32[]{:S(2)}, u32[]{:S(2)}) collective-permute-start(f32[3,384]{1,0:T(4,128)S(1)} %pad_maximum_fusion.5), channel_id=1, source_target_pairs={{0,2},{1,3},{2,0},{3,1},{4,6},{5,7},{6,4},{7,5},{8,10},{9,11},{10,... | collective-permute-start | bytes 13832 | tf_op jit(solution)/shard_map/ppermute | solution.py:9
  23.8 4.6 %collective-permute-start.6 = (f32[3,384]{1,0:T(4,128)S(1)}, f32[3,384]{1,0:T(4,128)S(1)}, u32[]{:S(2)}, u32[]{:S(2)}) collective-permute-start(f32[3,384]{1,0:T(4,128)S(1)} %pad_maximum_fusion.6), channel_id=1, source_target_pairs={{0,8},{1,9},{2,10},{3,11},{4,12},{5,13},{6,14},{7,15},{8,0},{9,1},... | collective-permute-start | bytes 13832 | tf_op jit(solution)/shard_map/ppermute | solution.py:9
  28.4 3.7 %collective-permute-start.7 = (f32[3,384]{1,0:T(4,128)S(1)}, f32[3,384]{1,0:T(4,128)S(1)}, u32[]{:S(2)}, u32[]{:S(2)}) collective-permute-start(f32[3,384]{1,0:T(4,128)S(1)} %pad_maximum_fusion.7), channel_id=1, source_target_pairs={{0,4},{1,5},{2,6},{3,7},{4,0},{5,1},{6,2},{7,3},{8,12},{9,13},{10,... | collective-permute-start | bytes 13832 | tf_op jit(solution)/shard_map/ppermute | solution.py:9
  30.0 5.7 %collective-permute-start.8 = (bf16[384,256]{1,0:T(8,128)(2,1)S(1)}, bf16[384,256]{1,0:T(8,128)(2,1)S(1)}, u32[]{:S(2)}, u32[]{:S(2)}) collective-permute-start(bf16[384,256]{1,0:T(8,128)(2,1)S(1)} %pad_maximum_fusion.1), channel_id=1, source_target_pairs={{0,2},{1,3},{2,0},{3,1},{4,6},{5,7},{6,4},{7,5},{8,10},{9,11},{10,... | collective-permute-start | bytes 589832 | tf_op jit(solution)/shard_map/ppermute | solution.py:9
  36.0 6.5 %collective-permute-start.9 = (bf16[192,256]{1,0:T(8,128)(2,1)S(1)}, bf16[192,256]{1,0:T(8,128)(2,1)S(1)}, u32[]{:S(2)}, u32[]{:S(2)}) collective-permute-start(bf16[192,256]{1,0:T(8,128)(2,1)S(1)} %pad_maximum_fusion.2), channel_id=1, source_target_pairs={{0,8},{1,9},{2,10},{3,11},{4,12},{5,13},{6,14},{7,15},{8,0},{9,1},... | collective-permute-start | bytes 294920 | tf_op jit(solution)/shard_map/ppermute | solution.py:9
  40.1 7.4 %collective-permute-start.11 = (f32[512,256]{1,0:T(8,128)S(1)}, f32[512,256]{1,0:T(8,128)S(1)}, u32[]{:S(2)}, u32[]{:S(2)}) collective-permute-start(f32[512,256]{1,0:T(8,128)S(1)} %slice.134), channel_id=1, source_target_pairs={{0,1},{1,0},{2,3},{3,2},{4,5},{5,4},{6,7},{7,6},{8,9},{9,8},{10,11... | collective-permute-start | bytes 1572872 | tf_op jit(solution)/shard_map/ppermute | solution.py:9
  42.7 4.7 %collective-permute-start.10 = (f32[96,256]{1,0:T(8,128)S(1)}, f32[96,256]{1,0:T(8,128)S(1)}, u32[]{:S(2)}, u32[]{:S(2)}) collective-permute-start(f32[96,256]{1,0:T(8,128)S(1)} %pad_maximum_fusion.3), channel_id=1, source_target_pairs={{0,4},{1,5},{2,6},{3,7},{4,0},{5,1},{6,2},{7,3},{8,12},{9,13},{10,... | collective-permute-start | bytes 294920 | tf_op jit(solution)/shard_map/ppermute | solution.py:9
  47.5 5.0 %collective-permute-start.12 = (bf16[256,256]{1,0:T(8,128)(2,1)S(1)}, bf16[256,256]{1,0:T(8,128)(2,1)S(1)}, u32[]{:S(2)}, u32[]{:S(2)}) collective-permute-start(bf16[256,256]{1,0:T(8,128)(2,1)S(1)} %slice.184), channel_id=1, source_target_pairs={{0,16},{16,0},{1,17},{17,1},{2,18},{18,2},{3,19},{19,3},{4,20},{20... | collective-permute-start | bytes 393224 | tf_op jit(solution)/shard_map/ppermute | solution.py:9
where the time goes:
time: 53.6 us; the launch traced here: 53.3 us
  starting transfers between devices  20.8 us (39%)
  waiting for transfers between devices  20.7 us (39%)
  other arithmetic  6.44 us (12%)
  matrix products  2.5 us (5%)
  local copies, waits for them, and re-layouts  1.91 us (4%)
  between operations  0.92 us (2%)
    ppermute x13, starting transfers between devices, swap(): return lax.ppermute(value, axis, [(i, i ^ mask) for i in range(count)])  20.8 us
    ppermute x13, waiting for transfers between devices, swap(): return lax.ppermute(value, axis, [(i, i ^ mask) for i in range(count)])  20.7 us
  transfers between devices with their start and end apart: 13, of which 9 were waited for; matrix products, arithmetic and copies ran while one was open for 13% of the time, Pallas kernels for 0%

commit v1 on v0

--- a/solution.py
+++ b/solution.py
@@ -21,6 +21,10 @@
     )
 
 
+def part(value, upper, size):
+    return lax.dynamic_slice_in_dim(value, upper * size, size, 0)
+
+
 def local(users, items, pos_ids):
     f32, bf16 = jnp.float32, jnp.bfloat16
     own, width = users.shape
@@ -29,12 +33,11 @@
     here = lax.axis_index("items")
     group = lax.axis_index("batch")
     steps = user_steps(count)
-    block = -(-(own + 1) // 16) * 16
+    block = -(-(own + 2) // 16) * 16
 
-    ids_row = jnp.concatenate(
-        [pos_ids // 256, pos_ids % 256, jnp.zeros((width - 2 * own,), jnp.int32)]
-    ).astype(bf16)
-    seen = jnp.concatenate([users, ids_row[None], jnp.zeros((block - own - 1, width), bf16)], 0)
+    ids_rows = jnp.stack([pos_ids // 256, pos_ids % 256])
+    ids_rows = jnp.pad(ids_rows, ((0, block - own - 2), (0, width - own))).astype(bf16)
+    seen = lax.optimization_barrier(jnp.concatenate([users, ids_rows], 0))
     half_bank = jnp.concatenate([items, swap(items, "batch", 1)], 0)
     for bit, mask in steps:
         theirs = swap(seen, "items", mask)
@@ -43,8 +46,8 @@
     rows = seen.shape[0]
     blocks = rows // block
 
-    pairs = seen.reshape(blocks, block, width)[:, own, : 2 * own].astype(jnp.int32)
-    ids = pairs[:, :own] * 256 + pairs[:, own:]
+    pairs = seen.reshape(blocks, block, width)[:, own : own + 2, :own].astype(jnp.int32)
+    ids = pairs[:, 0] * 256 + pairs[:, 1]
     owner = ids // per_bank
     at = owner % count
     slot = ((at ^ here) & 1) * 2 + ((owner // count) ^ group)
@@ -66,38 +69,28 @@
     )
     pick = jnp.dot(match.astype(bf16), bank, preferred_element_type=f32).astype(bf16)
 
+    place = 0
     for n, (bit, mask) in enumerate(reversed(steps)):
         upper = ((here & bit) != 0).astype(jnp.int32)
         half = acc.shape[0] // 2
         stats = swap(jnp.stack([peak, total, positive]), "items", mask)
-        give = (1 - upper) * half
         wire = f32 if n == len(steps) - 1 else bf16
-        sent = jnp.concatenate(
-            [
-                lax.dynamic_slice_in_dim(acc, give, half, 0).astype(wire),
-                lax.dynamic_slice_in_dim(pick, give, half, 0).astype(wire),
-            ],
-            0,
-        )
-        got = swap(sent, "items", mask)
+        sent = [part(acc, 1 - upper, half).astype(wire), part(pick, 1 - upper, half).astype(wire)]
+        got = swap(jnp.concatenate(sent, 0), "items", mask)
         top = jnp.maximum(peak, stats[0])
-        scale_mine = jnp.exp(peak - top)
-        scale_theirs = jnp.exp(stats[0] - top)
-        total = total * scale_mine + stats[1] * scale_theirs
+        mine = jnp.exp(peak - top)
+        theirs = jnp.exp(stats[0] - top)
+        total = total * mine + stats[1] * theirs
         positive = positive + stats[2]
         peak = top
-        keep = upper * half
-        base = keep if acc.shape[0] == rows else base + keep
-        mine = lax.dynamic_slice_in_dim(scale_mine, base, half, 0)
-        theirs = lax.dynamic_slice_in_dim(scale_theirs, base, half, 0)
-        acc = (
-            lax.dynamic_slice_in_dim(acc, keep, half, 0) * mine[:, None]
-            + got[:half].astype(f32) * theirs[:, None]
-        )
-        pick = lax.dynamic_slice_in_dim(pick, keep, half, 0) + got[half:].astype(bf16)
+        mine, theirs, peak = lax.optimization_barrier((mine, theirs, peak))
+        place = place * 2 + upper
+        mine, theirs = part(mine, place, half), part(theirs, place, half)
+        acc = part(acc, upper, half) * mine[:, None] + got[:half].astype(f32) * theirs[:, None]
+        pick = part(pick, upper, half) + got[half:].astype(bf16)
 
     lse = peak + jnp.log(total)
-    last = lambda v: lax.dynamic_slice_in_dim(v, base, block, 0)[:own]
+    last = lambda value: part(value, place, block)[:own]
     loss = last(lse) - last(positive)
     user_grad = acc[:own] / last(total)[:, None] - pick[:own].astype(f32)
 
@@ -106,7 +99,8 @@
     grad = lax.dot_general(weights, clean, (((0,), (0,)), ((), ())), preferred_element_type=f32)
     near = 2 * per_bank
     grad = grad[:near] + swap(grad[near:], "items", 1)
-    item_grad = grad[:per_bank] + swap(grad[per_bank:].astype(bf16), "batch", 1).astype(f32)
+    far = swap(grad[per_bank:].astype(bf16), "batch", 1)
+    item_grad = grad[:per_bank] + far.astype(f32)
     return (loss, user_grad, item_grad)
 
 

time: 53.6 us -> 52.7 us (0.983)
  other arithmetic: 6.44 us -> 5.46 us
    select_n x3, other arithmetic: 0.97 us -> 0.1 us  [doubled(): jnp.where(upper, jnp.concatenate([theirs, mine], 0), jnp.concatenate([min...]
    concatenate x5 -> x4, other arithmetic: 1.51 us -> 0.76 us  [the longest x1 0.73 us: local(): seen = lax.optimization_barrier(jnp.concatenate([users, ids_rows], 0))]
    another operation x0 -> x2, other arithmetic: none -> 0.68 us  [local(): ids_rows = jnp.stack([pos_ids // 256, pos_ids % 256])]
  transfers between devices with their start and end apart: 13 -> 13, of which waited for: 9 -> 9; matrix products, arithmetic and copies ran while one was open for 13% -> 11% of each run, Pallas kernels for 0% -> 0%
where the time goes in v1:
time: 52.7 us; the launch traced here: 52.4 us
  starting transfers between devices  20.9 us (40%)
  waiting for transfers between devices  20.7 us (39%)
  other arithmetic  5.46 us (10%)
  matrix products  2.5 us (5%)
  local copies, waits for them, and re-layouts  1.9 us (4%)
  between operations  0.97 us (2%)
    ppermute x13, starting transfers between devices, swap(): return lax.ppermute(value, axis, [(i, i ^ mask) for i in range(count)])  20.9 us
    ppermute x13, waiting for transfers between devices, swap(): return lax.ppermute(value, axis, [(i, i ^ mask) for i in range(count)])  20.7 us
  transfers between devices with their start and end apart: 13, of which 9 were waited for; matrix products, arithmetic and copies ran while one was open for 11% of the time, Pallas kernels for 0%

profile of v1, /device:TPU:0, one launch (start us, length us, event | category | flops | bytes accessed | tf_op | source)
XLA Modules:
  0.0 52.4 jit_solution(11550602946053319992)
XLA Ops:
  0.6 0.7 %convert_bitcast_fusion = (bf16[1,40]{1,0:T(2,128)(2,1)S(1)}, bf16[1,40]{1,0:T(2,128)(2,1)S(1)}) fusion(s32[40]{0:T(128)} %param.5), kind=kLoop, calls=%fused_computation.133 | loop fusion | flops 840 | bytes 320 | tf_op jit(solution)/shard_map/stack | solution.py:38
  1.3 0.7 %pad_maximum_fusion.4 = bf16[48,256]{1,0:T(8,128)(2,1)S(1)} fusion(bf16[8,256]{1,0:T(8,128)(2,1)S(1)} %fusion.31, bf16[40,256]{1,0:T(8,128)(2,1)} %param.3), kind=kLoop, calls=%fused_computation.44 | loop fusion | flops 49152 | bytes 49152 | tf_op jit(solution)/shard_map/concatenate | solution.py:40
  2.0 3.1 %collective-permute-start = (bf16[48,256]{1,0:T(8,128)(2,1)S(1)}, bf16[48,256]{1,0:T(8,128)(2,1)S(1)}, u32[]{:S(2)}, u32[]{:S(2)}) collective-permute-start(bf16[48,256]{1,0:T(8,128)(2,1)S(1)} %pad_maximum_fusion.4), channel_id=1, source_target_pairs={{0,4},{1,5},{2,6},{3,7},{4,0},{5,1},{6,2},{7,3},{8,12},{9,13},{10,... | collective-permute-start | bytes 73736 | tf_op jit(solution)/shard_map/ppermute | solution.py:9
  5.1 1.5 %collective-permute-start.3 = (bf16[256,256]{1,0:T(8,128)(2,1)}, bf16[256,256]{1,0:T(8,128)(2,1)S(1)}, u32[]{:S(2)}, u32[]{:S(2)}) collective-permute-start(bf16[256,256]{1,0:T(8,128)(2,1)} %param.4), channel_id=1, source_target_pairs={{0,16},{16,0},{1,17},{17,1},{2,18},{18,2},{3,19},{19,3},{4,20},{20... | collective-permute-start | bytes 393224 | tf_op jit(solution)/shard_map/ppermute | solution.py:9
  6.6 0.9 %constant_dynamic-update-slice_fusion.2 = bf16[1024,256]{1,0:T(8,128)(2,1)S(1)} fusion(bf16[256,256]{1,0:T(8,128)(2,1)} %param.4), kind=kLoop, calls=%fused_computation.54 | loop fusion | bytes 262144
  7.6 2.7 %collective-permute-start.1 = (bf16[96,256]{1,0:T(8,128)(2,1)S(1)}, bf16[96,256]{1,0:T(8,128)(2,1)S(1)}, u32[]{:S(2)}, u32[]{:S(2)}) collective-permute-start(bf16[96,256]{1,0:T(8,128)(2,1)S(1)} %maximum_select_fusion.2), channel_id=1, source_target_pairs={{0,8},{1,9},{2,10},{3,11},{4,12},{5,13},{6,14},{7,15},{8,0},{9,1},... | collective-permute-start | bytes 147464 | tf_op jit(solution)/shard_map/ppermute | solution.py:9
  10.2 2.4 %collective-permute-done.1 = bf16[96,256]{1,0:T(8,128)(2,1)S(1)} collective-permute-done((bf16[96,256]{1,0:T(8,128)(2,1)S(1)}, bf16[96,256]{1,0:T(8,128)(2,1)S(1)}, u32[]{:S(2)}, u32[]{:S(2)}) %collective-permute-start.1) | collective-permute-done | bytes 49184 | tf_op jit(solution)/shard_map/ppermute | solution.py:9
  12.7 1.6 %collective-permute-start.2 = (bf16[192,256]{1,0:T(8,128)(2,1)S(1)}, bf16[192,256]{1,0:T(8,128)(2,1)S(1)}, u32[]{:S(2)}, u32[]{:S(2)}) collective-permute-start(bf16[192,256]{1,0:T(8,128)(2,1)S(1)} %maximum_select_fusion.1), channel_id=1, source_target_pairs={{0,2},{1,3},{2,0},{3,1},{4,6},{5,7},{6,4},{7,5},{8,10},{9,11},{10,... | collective-permute-start | bytes 294920 | tf_op jit(solution)/shard_map/ppermute | solution.py:9
  14.2 0.9 %pad_maximum_fusion = bf16[512,256]{1,0:T(8,128)(2,1)S(1)} fusion(bf16[256,256]{1,0:T(8,128)(2,1)S(1)} %collective-permute-done.3, bf16[256,256]{1,0:T(8,128)(2,1)} %param.4), kind=kLoop, calls=%fused_computation.22 | loop fusion | flops 524288 | bytes 524288 | tf_op jit(solution)/shard_map/concatenate | solution.py:41
  15.3 2.1 %collective-permute-done.2 = bf16[192,256]{1,0:T(8,128)(2,1)S(1)} collective-permute-done((bf16[192,256]{1,0:T(8,128)(2,1)S(1)}, bf16[192,256]{1,0:T(8,128)(2,1)S(1)}, u32[]{:S(2)}, u32[]{:S(2)}) %collective-permute-start.2) | collective-permute-done | bytes 98336 | tf_op jit(solution)/shard_map/ppermute | solution.py:9
  17.6 0.5 fusion.52
  18.1 0.4 fusion.5
  18.5 0.5 fusion.2
  19.1 1.6 %collective-permute-start.5 = (f32[3,384]{1,0:T(4,128)S(1)}, f32[3,384]{1,0:T(4,128)S(1)}, u32[]{:S(2)}, u32[]{:S(2)}) collective-permute-start(f32[3,384]{1,0:T(4,128)S(1)} %pad_maximum_fusion.5), channel_id=1, source_target_pairs={{0,2},{1,3},{2,0},{3,1},{4,6},{5,7},{6,4},{7,5},{8,10},{9,11},{10,... | collective-permute-start | bytes 13832 | tf_op jit(solution)/shard_map/ppermute | solution.py:9
  20.7 0.4 convolution_add_fusion
  21.1 0.4 fusion.3
  21.5 1.2 %collective-permute-done.5 = f32[3,384]{1,0:T(4,128)S(1)} collective-permute-done((f32[3,384]{1,0:T(4,128)S(1)}, f32[3,384]{1,0:T(4,128)S(1)}, u32[]{:S(2)}, u32[]{:S(2)}) %collective-permute-start.5) | collective-permute-done | bytes 4640 | tf_op jit(solution)/shard_map/ppermute | solution.py:9
  22.9 2.8 %collective-permute-start.6 = (f32[3,384]{1,0:T(4,128)S(1)}, f32[3,384]{1,0:T(4,128)S(1)}, u32[]{:S(2)}, u32[]{:S(2)}) collective-permute-start(f32[3,384]{1,0:T(4,128)S(1)} %pad_maximum_fusion.6), channel_id=1, source_target_pairs={{0,8},{1,9},{2,10},{3,11},{4,12},{5,13},{6,14},{7,15},{8,0},{9,1},... | collective-permute-start | bytes 13832 | tf_op jit(solution)/shard_map/ppermute | solution.py:9
  25.6 1.8 %collective-permute-done.6 = f32[3,384]{1,0:T(4,128)S(1)} collective-permute-done((f32[3,384]{1,0:T(4,128)S(1)}, f32[3,384]{1,0:T(4,128)S(1)}, u32[]{:S(2)}, u32[]{:S(2)}) %collective-permute-start.6) | collective-permute-done | bytes 4640 | tf_op jit(solution)/shard_map/ppermute | solution.py:9
  27.5 1.6 %collective-permute-start.7 = (f32[3,384]{1,0:T(4,128)S(1)}, f32[3,384]{1,0:T(4,128)S(1)}, u32[]{:S(2)}, u32[]{:S(2)}) collective-permute-start(f32[3,384]{1,0:T(4,128)S(1)} %pad_maximum_fusion.7), channel_id=1, source_target_pairs={{0,4},{1,5},{2,6},{3,7},{4,0},{5,1},{6,2},{7,3},{8,12},{9,13},{10,... | collective-permute-start | bytes 13832 | tf_op jit(solution)/shard_map/ppermute | solution.py:9
  29.2 1.6 %collective-permute-start.8 = (bf16[384,256]{1,0:T(8,128)(2,1)S(1)}, bf16[384,256]{1,0:T(8,128)(2,1)S(1)}, u32[]{:S(2)}, u32[]{:S(2)}) collective-permute-start(bf16[384,256]{1,0:T(8,128)(2,1)S(1)} %pad_maximum_fusion.1), channel_id=1, source_target_pairs={{0,2},{1,3},{2,0},{3,1},{4,6},{5,7},{6,4},{7,5},{8,10},{9,11},{10,... | collective-permute-start | bytes 589832 | tf_op jit(solution)/shard_map/ppermute | solution.py:9
  31.1 0.1 collective-permute-done.7
  31.3 3.6 %collective-permute-done.8 = bf16[384,256]{1,0:T(8,128)(2,1)S(1)} collective-permute-done((bf16[384,256]{1,0:T(8,128)(2,1)S(1)}, bf16[384,256]{1,0:T(8,128)(2,1)S(1)}, u32[]{:S(2)}, u32[]{:S(2)}) %collective-permute-start.8) | collective-permute-done | bytes 196640 | tf_op jit(solution)/shard_map/ppermute | solution.py:9
  35.1 3.0 %collective-permute-start.9 = (bf16[192,256]{1,0:T(8,128)(2,1)S(1)}, bf16[192,256]{1,0:T(8,128)(2,1)S(1)}, u32[]{:S(2)}, u32[]{:S(2)}) collective-permute-start(bf16[192,256]{1,0:T(8,128)(2,1)S(1)} %pad_maximum_fusion.2), channel_id=1, source_target_pairs={{0,8},{1,9},{2,10},{3,11},{4,12},{5,13},{6,14},{7,15},{8,0},{9,1},... | collective-permute-start | bytes 294920 | tf_op jit(solution)/shard_map/ppermute | solution.py:9
  38.1 0.7 %fusion.6 = f32[1024,256]{1,0:T(8,128)S(1)} fusion(f32[384,1024]{1,0:T(8,128)S(1)} %get-tuple-element.48, f32[384]{0:T(512)S(1)} %get-tuple-element.32, s32[384]{0:T(512)S(1)} %eq.30, bf16[384,256]{1,0:T(8,128)(2,1)S(1)} %maximum_select_fusion, pred[384]{0:T(512)(128)(4,1)S(1)} %fusion.38), kind=kOutput, calls=%fused_computation.11 | convolution fusion | flops 203390976 | bytes 2821504 | tf_op jit(solution)/shard_map/dot_general | solution.py:99
  39.1 2.6 %collective-permute-done.9 = bf16[192,256]{1,0:T(8,128)(2,1)S(1)} collective-permute-done((bf16[192,256]{1,0:T(8,128)(2,1)S(1)}, bf16[192,256]{1,0:T(8,128)(2,1)S(1)}, u32[]{:S(2)}, u32[]{:S(2)}) %collective-permute-start.9) | collective-permute-done | bytes 98336 | tf_op jit(solution)/shard_map/ppermute | solution.py:9
  41.9 0.5 slice_subtract_fusion
  42.7 3.9 %collective-permute-done.10 = f32[96,256]{1,0:T(8,128)S(1)} collective-permute-done((f32[96,256]{1,0:T(8,128)S(1)}, f32[96,256]{1,0:T(8,128)S(1)}, u32[]{:S(2)}, u32[]{:S(2)}) %collective-permute-start.10) | collective-permute-done | bytes 98336 | tf_op jit(solution)/shard_map/ppermute | solution.py:9
  46.7 1.3 %collective-permute-start.12 = (bf16[256,256]{1,0:T(8,128)(2,1)S(1)}, bf16[256,256]{1,0:T(8,128)(2,1)S(1)}, u32[]{:S(2)}, u32[]{:S(2)}) collective-permute-start(bf16[256,256]{1,0:T(8,128)(2,1)S(1)} %slice.178), channel_id=1, source_target_pairs={{0,16},{16,0},{1,17},{17,1},{2,18},{18,2},{3,19},{19,3},{4,20},{20... | collective-permute-start | bytes 393224 | tf_op jit(solution)/shard_map/ppermute | solution.py:9
  48.0 0.7 %fusion.19 = f32[40,256]{1,0:T(8,128)} fusion(f32[48,256]{1,0:T(8,128)S(1)} %slice.129, f32[96,256]{1,0:T(8,128)S(1)} %multiply_add_fusion.1, s32[]{:T(128)S(6)} %mul.156, bf16[48,256]{1,0:T(8,128)(2,1)S(1)} %slice.133, bf16[96,256]{1,0:T(8,128)(2,1)S(1)} %slice_add_fusion.3, f32[40]{0:T(128)S(1)} %bitcast.16, f32[40]{0:T(128)S(1)} %bitcast.17, ...), kind=kLoop, calls=%fused_computation.42 | loop fusion | flops 92160 | bytes 164324 | tf_op jit(solution)/shard_map/sub | solution.py:95
  48.7 3.0 %collective-permute-done.12 = bf16[256,256]{1,0:T(8,128)(2,1)S(1)} collective-permute-done((bf16[256,256]{1,0:T(8,128)(2,1)S(1)}, bf16[256,256]{1,0:T(8,128)(2,1)S(1)}, u32[]{:S(2)}, u32[]{:S(2)}) %collective-permute-start.12) | collective-permute-done | bytes 131104 | tf_op jit(solution)/shard_map/ppermute | solution.py:9
  51.7 0.7 %slice_add_fusion.1 = f32[256,256]{1,0:T(8,128)} fusion(f32[512,256]{1,0:T(8,128)S(1)} %slice_add_fusion, bf16[256,256]{1,0:T(8,128)(2,1)S(1)} %collective-permute-done.12), kind=kLoop, calls=%fused_computation.21 | loop fusion | flops 131072 | bytes 655360 | tf_op jit(solution)/shard_map/add | solution.py:103
  (63 shorter events, 1.9 us)
Async XLA Ops:
  2.0 5.5 %collective-permute-start = (bf16[48,256]{1,0:T(8,128)(2,1)S(1)}, bf16[48,256]{1,0:T(8,128)(2,1)S(1)}, u32[]{:S(2)}, u32[]{:S(2)}) collective-permute-start(bf16[48,256]{1,0:T(8,128)(2,1)S(1)} %pad_maximum_fusion.4), channel_id=1, source_target_pairs={{0,4},{1,5},{2,6},{3,7},{4,0},{5,1},{6,2},{7,3},{8,12},{9,13},{10,... | collective-permute-start | bytes 73736 | tf_op jit(solution)/shard_map/ppermute | solution.py:9
  5.1 9.1 %collective-permute-start.3 = (bf16[256,256]{1,0:T(8,128)(2,1)}, bf16[256,256]{1,0:T(8,128)(2,1)S(1)}, u32[]{:S(2)}, u32[]{:S(2)}) collective-permute-start(bf16[256,256]{1,0:T(8,128)(2,1)} %param.4), channel_id=1, source_target_pairs={{0,16},{16,0},{1,17},{17,1},{2,18},{18,2},{3,19},{19,3},{4,20},{20... | collective-permute-start | bytes 393224 | tf_op jit(solution)/shard_map/ppermute | solution.py:9
  7.6 5.1 %collective-permute-start.1 = (bf16[96,256]{1,0:T(8,128)(2,1)S(1)}, bf16[96,256]{1,0:T(8,128)(2,1)S(1)}, u32[]{:S(2)}, u32[]{:S(2)}) collective-permute-start(bf16[96,256]{1,0:T(8,128)(2,1)S(1)} %maximum_select_fusion.2), channel_id=1, source_target_pairs={{0,8},{1,9},{2,10},{3,11},{4,12},{5,13},{6,14},{7,15},{8,0},{9,1},... | collective-permute-start | bytes 147464 | tf_op jit(solution)/shard_map/ppermute | solution.py:9
  12.7 4.7 %collective-permute-start.2 = (bf16[192,256]{1,0:T(8,128)(2,1)S(1)}, bf16[192,256]{1,0:T(8,128)(2,1)S(1)}, u32[]{:S(2)}, u32[]{:S(2)}) collective-permute-start(bf16[192,256]{1,0:T(8,128)(2,1)S(1)} %maximum_select_fusion.1), channel_id=1, source_target_pairs={{0,2},{1,3},{2,0},{3,1},{4,6},{5,7},{6,4},{7,5},{8,10},{9,11},{10,... | collective-permute-start | bytes 294920 | tf_op jit(solution)/shard_map/ppermute | solution.py:9
  15.2 2.4 %collective-permute-start.4 = (bf16[512,256]{1,0:T(8,128)(2,1)S(1)}, bf16[512,256]{1,0:T(8,128)(2,1)S(1)}, u32[]{:S(2)}, u32[]{:S(2)}) collective-permute-start(bf16[512,256]{1,0:T(8,128)(2,1)S(1)} %pad_maximum_fusion), channel_id=1, source_target_pairs={{0,1},{1,0},{2,3},{3,2},{4,5},{5,4},{6,7},{7,6},{8,9},{9,8},{10,11... | collective-permute-start | bytes 786440 | tf_op jit(solution)/shard_map/ppermute | solution.py:9
  19.1 3.7 %collective-permute-start.5 = (f32[3,384]{1,0:T(4,128)S(1)}, f32[3,384]{1,0:T(4,128)S(1)}, u32[]{:S(2)}, u32[]{:S(2)}) collective-permute-start(f32[3,384]{1,0:T(4,128)S(1)} %pad_maximum_fusion.5), channel_id=1, source_target_pairs={{0,2},{1,3},{2,0},{3,1},{4,6},{5,7},{6,4},{7,5},{8,10},{9,11},{10,... | collective-permute-start | bytes 13832 | tf_op jit(solution)/shard_map/ppermute | solution.py:9
  22.9 4.6 %collective-permute-start.6 = (f32[3,384]{1,0:T(4,128)S(1)}, f32[3,384]{1,0:T(4,128)S(1)}, u32[]{:S(2)}, u32[]{:S(2)}) collective-permute-start(f32[3,384]{1,0:T(4,128)S(1)} %pad_maximum_fusion.6), channel_id=1, source_target_pairs={{0,8},{1,9},{2,10},{3,11},{4,12},{5,13},{6,14},{7,15},{8,0},{9,1},... | collective-permute-start | bytes 13832 | tf_op jit(solution)/shard_map/ppermute | solution.py:9
  27.5 3.7 %collective-permute-start.7 = (f32[3,384]{1,0:T(4,128)S(1)}, f32[3,384]{1,0:T(4,128)S(1)}, u32[]{:S(2)}, u32[]{:S(2)}) collective-permute-start(f32[3,384]{1,0:T(4,128)S(1)} %pad_maximum_fusion.7), channel_id=1, source_target_pairs={{0,4},{1,5},{2,6},{3,7},{4,0},{5,1},{6,2},{7,3},{8,12},{9,13},{10,... | collective-permute-start | bytes 13832 | tf_op jit(solution)/shard_map/ppermute | solution.py:9
  29.2 5.7 %collective-permute-start.8 = (bf16[384,256]{1,0:T(8,128)(2,1)S(1)}, bf16[384,256]{1,0:T(8,128)(2,1)S(1)}, u32[]{:S(2)}, u32[]{:S(2)}) collective-permute-start(bf16[384,256]{1,0:T(8,128)(2,1)S(1)} %pad_maximum_fusion.1), channel_id=1, source_target_pairs={{0,2},{1,3},{2,0},{3,1},{4,6},{5,7},{6,4},{7,5},{8,10},{9,11},{10,... | collective-permute-start | bytes 589832 | tf_op jit(solution)/shard_map/ppermute | solution.py:9
  35.1 6.6 %collective-permute-start.9 = (bf16[192,256]{1,0:T(8,128)(2,1)S(1)}, bf16[192,256]{1,0:T(8,128)(2,1)S(1)}, u32[]{:S(2)}, u32[]{:S(2)}) collective-permute-start(bf16[192,256]{1,0:T(8,128)(2,1)S(1)} %pad_maximum_fusion.2), channel_id=1, source_target_pairs={{0,8},{1,9},{2,10},{3,11},{4,12},{5,13},{6,14},{7,15},{8,0},{9,1},... | collective-permute-start | bytes 294920 | tf_op jit(solution)/shard_map/ppermute | solution.py:9
  39.0 7.5 %collective-permute-start.11 = (f32[512,256]{1,0:T(8,128)S(1)}, f32[512,256]{1,0:T(8,128)S(1)}, u32[]{:S(2)}, u32[]{:S(2)}) collective-permute-start(f32[512,256]{1,0:T(8,128)S(1)} %slice.136), channel_id=1, source_target_pairs={{0,1},{1,0},{2,3},{3,2},{4,5},{5,4},{6,7},{7,6},{8,9},{9,8},{10,11... | collective-permute-start | bytes 1572872 | tf_op jit(solution)/shard_map/ppermute | solution.py:9
  41.9 4.7 %collective-permute-start.10 = (f32[96,256]{1,0:T(8,128)S(1)}, f32[96,256]{1,0:T(8,128)S(1)}, u32[]{:S(2)}, u32[]{:S(2)}) collective-permute-start(f32[96,256]{1,0:T(8,128)S(1)} %pad_maximum_fusion.3), channel_id=1, source_target_pairs={{0,4},{1,5},{2,6},{3,7},{4,0},{5,1},{6,2},{7,3},{8,12},{9,13},{10,... | collective-permute-start | bytes 294920 | tf_op jit(solution)/shard_map/ppermute | solution.py:9
  46.7 5.0 %collective-permute-start.12 = (bf16[256,256]{1,0:T(8,128)(2,1)S(1)}, bf16[256,256]{1,0:T(8,128)(2,1)S(1)}, u32[]{:S(2)}, u32[]{:S(2)}) collective-permute-start(bf16[256,256]{1,0:T(8,128)(2,1)S(1)} %slice.178), channel_id=1, source_target_pairs={{0,16},{16,0},{1,17},{17,1},{2,18},{18,2},{3,19},{19,3},{4,20},{20... | collective-permute-start | bytes 393224 | tf_op jit(solution)/shard_map/ppermute | solution.py:9
